TPU v7x, 256 devices: a whole 4x4x8 slice. The times are simulated.
256 devices in a mesh: dp: 16 (over y, x), expert: 8 (over z), tensor: 2 (over core).
Axes of the slice: x: 4, y: 4, z: 8, core: 2. Of those that a mesh axis runs over, the one named last changes fastest.
Arguments:
- tokens: bfloat16 [2048, 4096], P(('dp', 'expert'), 'tensor'), may hold values from -6 to 6
- target: bfloat16 [2048, 4096], P(('dp', 'expert'), 'tensor'), may hold values from -4 to 4
- router: bfloat16 [4096, 8], P('tensor'), may hold values from -1 to 1
- w_gate: bfloat16 [8, 4096, 14336], P('expert', None, ('dp', 'tensor')), may hold values from -1 to 1
- w_up: bfloat16 [8, 4096, 14336], P('expert', None, ('dp', 'tensor')), may hold values from -1 to 1
- w_down: bfloat16 [8, 14336, 4096], P('expert', ('dp', 'tensor')), may hold values from -1 to 1
- expert_ids: int32 [2048, 2], P(('dp', 'expert')), may hold values from 0 to 7, as said below
- lengths: int32 [64], replicated, may hold values from 1 to 128, 2048 in all
- bench_ids: int32 [64], replicated, may hold values from 0 to 15
Outputs:
- mixed: bfloat16 [2048, 4096], P(('dp', 'expert'), 'tensor')
- bench_loss: float32 [16], replicated
- counts: int32 [16], replicated
Inputs may be any that keep to these rules, and one draw needn't show every extreme that they name: `expert_ids`: each row names two different experts; among the 16 rows of one device no expert is named by more than 8 rows; for each index of dp, one expert is named by exactly 8 rows of every device of that index. The lengths sum to 2048.
All inputs are finite; a program needn't handle non-finite values.
Results may differ from a plain program's by a relative error of at most 0.0085.
Values may be sent and summed in bfloat16 or wider, within the bound.
A program may use at most 128 MiB of HBM per device.

v0:
```python
import jax
import jax.numpy as jnp
from jax import lax
from jax.sharding import Mesh
from jax.sharding import PartitionSpec as P

D = 4096
NB = 16
CAP = 8
DP = ("dp_0", "dp_1")
DP_EXPERT = ("dp_0", "dp_1", "expert")
DP_EXPERT_TENSOR = ("dp_0", "dp_1", "expert", "tensor")
DP_TENSOR = ("dp_0", "dp_1", "tensor")


def cut_along(shard, dim, size):
    before, after = (shard.shape[:dim], shard.shape[dim + 1 :])
    return jnp.moveaxis(shard.reshape(*before, size, -1, *after), dim, 0)


def sent_and_summed(shard, axis, dim):
    pieces = cut_along(shard, dim, lax.axis_size(axis))
    arrived = lax.all_to_all(pieces, axis, split_axis=0, concat_axis=0, tiled=True)
    return arrived.sum(axis=0)


def one_axis_at_a_time(shard, axes):
    for axis in axes:
        shard = lax.psum(shard, axis)
    return shard


def per_device(tokens, target, router, w_gate, w_up, w_down, expert_ids, lengths, bench_ids):
    tensor_count = lax.axis_size("tensor")
    local_tokens = tokens.shape[0]
    experts = router.shape[1]
    half_cap = CAP // tensor_count
    slot_rows = tensor_count * experts * half_cap
    partial_value = jnp.dot(tokens, router, preferred_element_type=jnp.float32)
    logits = lax.psum(partial_value, "tensor")
    chosen = expert_ids[:, :, None] == jnp.arange(experts, dtype=jnp.int32)[None, None, :]
    picked = jnp.sum(jnp.where(chosen, logits[:, None, :], jnp.float32(0.0)), axis=2)
    gates = jnp.stack(
        [jax.nn.sigmoid(picked[:, 0] - picked[:, 1]), jax.nn.sigmoid(picked[:, 1] - picked[:, 0])],
        axis=1,
    )
    marks = chosen.reshape(local_tokens * 2, experts).astype(jnp.int32)
    before = jnp.cumsum(marks, axis=0) - marks
    slot = jnp.sum(before * marks, axis=1)
    flat_ids = expert_ids.reshape(local_tokens * 2)
    target_row = slot // half_cap * (experts * half_cap) + flat_ids * half_cap + slot % half_cap
    placing = (target_row[None, :] == jnp.arange(slot_rows, dtype=jnp.int32)[:, None]).reshape(
        slot_rows, local_tokens, 2
    )
    dispatch_map = jnp.any(placing, axis=2).astype(jnp.bfloat16)
    outgoing = jnp.dot(dispatch_map, tokens, preferred_element_type=jnp.float32).astype(
        jnp.bfloat16
    )
    outgoing = outgoing.reshape(tensor_count, experts, half_cap, tokens.shape[1])
    arrived = lax.all_to_all(outgoing, "expert", split_axis=1, concat_axis=1, tiled=True)
    whole = lax.all_gather(arrived, "tensor", axis=3, tiled=True)
    whole = whole.reshape(1, slot_rows, D)
    every_row = lax.all_gather(whole, DP, axis=0, tiled=True).reshape(-1, D)
    gate_w = w_gate[0]
    up_w = w_up[0]
    down_w = w_down[0]
    gate = jnp.dot(every_row, gate_w, preferred_element_type=jnp.float32)
    up = jnp.dot(every_row, up_w, preferred_element_type=jnp.float32)
    hidden = (jax.nn.silu(gate) * up).astype(jnp.bfloat16)
    summed = lax.psum_scatter(
        jnp.dot(hidden, down_w, preferred_element_type=jnp.float32),
        DP,
        scatter_dimension=0,
        tiled=True,
    )
    summed = sent_and_summed(summed, "tensor", 1)
    results = summed.astype(jnp.bfloat16).reshape(
        tensor_count, experts, half_cap, D // tensor_count
    )
    returned = lax.all_to_all(results, "expert", split_axis=1, concat_axis=1, tiled=True)
    weights = jnp.einsum("rtk,tk->tr", placing.astype(jnp.float32), gates)
    flat_back = returned.reshape(slot_rows, -1).astype(jnp.float32)
    mixed = jnp.dot(weights, flat_back, precision=lax.Precision.HIGHEST).astype(jnp.bfloat16)
    first_index = lax.axis_index(DP_EXPERT) * local_tokens
    position = first_index + jnp.arange(local_tokens, dtype=jnp.int32)
    ends = jnp.cumsum(lengths)
    starts = ends - lengths
    inside = ((position[:, None] >= starts[None, :]) & (position[:, None] < ends[None, :])).astype(
        jnp.float32
    )
    closing = jnp.any((position + 1)[:, None] == ends[None, :], axis=1)
    scored = jnp.where(closing, jnp.float32(0.0), jnp.float32(1.0))
    bench_table = bench_ids[:, None] == jnp.arange(NB, dtype=jnp.int32)[None, :]
    bench_of = jnp.dot(inside, bench_table.astype(jnp.float32), precision=lax.Precision.HIGHEST)
    diff = mixed.astype(jnp.float32) - target.astype(jnp.float32)
    token_part = jnp.sum(diff * diff, axis=1) / D
    local_sums = jnp.dot(scored * token_part, bench_of, precision=lax.Precision.HIGHEST)
    loss_sum = one_axis_at_a_time(local_sums, DP_EXPERT_TENSOR)
    counts = jnp.sum(jnp.where(bench_table, (lengths - 1)[:, None], 0), axis=0)
    bench_loss = loss_sum / jnp.maximum(counts, 1).astype(jnp.float32)
    return (mixed, bench_loss, counts)


def solution(mesh):
    split = Mesh(
        mesh.devices.reshape(4, 4, mesh.shape["expert"], mesh.shape["tensor"]),
        ("dp_0", "dp_1", "expert", "tensor"),
    )
    in_specs = (
        P(DP_EXPERT, "tensor"),
        P(DP_EXPERT, "tensor"),
        P("tensor", None),
        P("expert", None, DP_TENSOR),
        P("expert", None, DP_TENSOR),
        P("expert", DP_TENSOR, None),
        P(DP_EXPERT, None),
        P(),
        P(),
    )
    out_specs = (P(DP_EXPERT, "tensor"), P(), P())
    return jax.shard_map(
        per_device, mesh=split, in_specs=in_specs, out_specs=out_specs, check_vma=False
    )
```

profile of v0, /device:TPU:1, one launch (start us, length us, event | category | flops | bytes accessed | tf_op | source)
XLA Modules:
  0.0 317.1 jit_solution(9953797493856227956)
XLA Ops:
  7.2 0.0 copy-start
  7.2 0.0 all-gather.2.cloned.1.call-start
  7.2 0.8 copy.53
  8.0 0.1 eq.64
  8.1 0.1 fusion.13
  8.1 0.1 reduce_window_sum.18
  8.2 0.2 select_reduce_fusion
  8.4 0.1 reduce_sum.48
  8.5 0.1 copy.54
  8.6 0.7 fusion.22
  9.3 0.1 fusion.34
  9.3 0.0 copy-done
  9.4 0.3 convolution_convert_fusion
  9.6 0.1 reshape.108
  9.7 0.1 copy.58
  9.8 19.3 %all_to_all.15 = bf16[2,8,4,2048]{3,2,0,1:T(4,128)(2,1)S(1)} all-to-all(bf16[2,8,4,2048]{3,2,0,1:T(4,128)(2,1)S(1)} %copy.58), channel_id=1, replica_groups=mesh['dp_0'=4,'dp_1'=4,'expert'=8,'tensor'=2] {'expert'}, dimensions={1} | all-to-all | bytes 524288 | tf_op jit(solution)/shard_map/all_to_all | solution.py:60
  29.2 4.1 %all_gather.6 = bf16[2,8,4,4096]{3,2,0,1:T(4,128)(2,1)S(1)} all-gather(bf16[2,8,4,2048]{3,2,0,1:T(4,128)(2,1)S(1)} %all_to_all.15), channel_id=1, replica_groups=mesh['dp_0'=4,'dp_1'=4,'expert'=8,'tensor'=2] {'tensor'}, dimensions={3}, use_global_device_ids=true | all-gather | bytes 786432 | tf_op jit(solution)/shard_map/all_gather | solution.py:61
  33.3 0.2 copy.59
  33.5 0.9 reshape.109
  34.4 0.0 all-gather.2.cloned.1.call-update
  34.4 0.0 reduce-scatter.2.cloned.1.call-start
  34.5 71.8 %all-gather.2.cloned.1.call-done = bf16[16,64,4096]{2,1,0:T(8,128)(2,1)} async-done(((bf16[1,64,4096]{2,1,0:T(8,128)(2,1)}), bf16[16,64,4096]{2,1,0:T(8,128)(2,1)}) %all-gather.2.cloned.1.call-update) | async-done | bytes 8388624 | tf_op jit(solution)/shard_map/all_gather | solution.py:63
  106.3 7.5 %fusion.4 = f32[1024,448]{0,1:T(8,128)S(1)} fusion(bf16[1024,4096]{1,0:T(8,128)(2,1)} %bitcast.45, bf16[1,4096,448]{1,2,0:T(8,128)(2,1)} %param.12), kind=kOutput, calls=%fused_computation.4 | convolution fusion | flops 3758096384 | bytes 13893632 | tf_op jit(solution)/shard_map/dot_general | solution.py:67
  113.8 16.5 %fusion = f32[1024,4096]{1,0:T(8,128)} fusion(bf16[1,448,4096]{2,1,0:T(8,128)(2,1)} %param.14, f32[1024,448]{0,1:T(8,128)S(1)} %fusion.4, bf16[1024,4096]{1,0:T(8,128)(2,1)} %bitcast.46, bf16[1,4096,448]{1,2,0:T(8,128)(2,1)} %param.13), kind=kOutput, calls=%fused_computation | convolution fusion | flops 7518945280 | bytes 34340864 | tf_op jit(solution)/shard_map/dot_general | solution.py:71
  130.3 0.0 copy-start.4
  130.3 0.0 copy-start.2
  130.3 0.0 copy-start.5
  130.3 0.0 copy-start.3
  130.3 0.0 reduce-scatter.2.cloned.1.call-update
  130.4 0.6 copy-done.4
  131.0 0.1 copy.63
  131.1 0.1 reduce-window.8
  131.2 0.1 reduce
  131.3 0.0 copy-done.2
  131.3 0.1 fusion.35
  131.4 3.0 psum.35
  134.4 0.0 copy-done.5
  134.4 0.1 select_reduce_fusion.1
  134.5 0.0 copy-done.3
  134.5 0.0 copy-start.6
  134.5 0.2 compare_reduce_fusion
  134.7 111.3 %reduce-scatter.2.cloned.1.call-done = f32[64,4096]{1,0:T(8,128)} async-done(((f32[1024,4096]{1,0:T(8,128)}), f32[64,4096]{1,0:T(8,128)}) %reduce-scatter.2.cloned.1.call-update) | async-done | bytes 1048592 | tf_op jit(solution)/shard_map/reduce_scatter | solution.py:70
  246.0 0.0 copy-start.1
  246.0 1.3 copy.71
  247.3 5.1 %all_to_all.16 = f32[2,64,2048]{2,1,0:T(8,128)S(1)} all-to-all(f32[2,64,2048]{2,1,0:T(8,128)S(1)} %bitcast.41), channel_id=1, replica_groups=mesh['dp_0'=4,'dp_1'=4,'expert'=8,'tensor'=2] {'tensor'}, dimensions={0} | all-to-all | bytes 2097152 | tf_op jit(solution)/shard_map/all_to_all | solution.py:23
  252.4 0.1 reduce_sum.50
  252.5 0.1 convert_element_type.37
  252.6 0.8 copy.61
  253.4 6.8 %all-to-all-start.2 = ((bf16[2,8,4,2048]{3,2,0,1:T(4,128)(2,1)}), bf16[2,8,4,2048]{3,2,0,1:T(4,128)(2,1)S(1)}, u32[]{:S(2)}, u32[]{:S(2)}) async-start(bf16[2,8,4,2048]{3,2,0,1:T(4,128)(2,1)} %copy.61), calls=%async_computation.3 | async-start | bytes 524288 | tf_op jit(solution)/shard_map/all_to_all | solution.py:80
  260.2 0.1 copy.65
  260.3 0.2 fusion.14
  260.5 0.1 fusion.11
  260.6 10.7 %all-to-all-done.2 = bf16[2,8,4,2048]{3,2,0,1:T(4,128)(2,1)S(1)} async-done(((bf16[2,8,4,2048]{3,2,0,1:T(4,128)(2,1)}), bf16[2,8,4,2048]{3,2,0,1:T(4,128)(2,1)S(1)}, u32[]{:S(2)}, u32[]{:S(2)}) %all-to-all-start.2) | async-done | bytes 262176 | tf_op jit(solution)/shard_map/all_to_all | solution.py:80
  271.3 0.1 copy.62
  271.4 0.1 reshape.112
  271.5 0.0 copy-done.1
  271.5 1.0 multiply_reduce_fusion
  272.4 0.1 convolution_bitcast_fusion
  272.6 8.0 %psum.36 = f32[16]{0:T(128)S(1)} all-reduce(f32[16]{0:T(128)S(1)} %convolution_bitcast_fusion), channel_id=1, replica_groups=mesh['dp_0'=4,'dp_1'=4,'expert'=8,'tensor'=2] {'dp_0'}, use_global_device_ids=true, to_apply=%region_10.11 | all-reduce | flops 16 | bytes 128 | tf_op jit(solution)/shard_map/psum | solution.py:29
  280.5 6.7 %psum.37 = f32[16]{0:T(128)S(1)} all-reduce(f32[16]{0:T(128)S(1)} %psum.36), channel_id=1, replica_groups=mesh['dp_0'=4,'dp_1'=4,'expert'=8,'tensor'=2] {'dp_1'}, use_global_device_ids=true, to_apply=%region_11.12 | all-reduce | flops 16 | bytes 128 | tf_op jit(solution)/shard_map/psum | solution.py:29
  287.2 10.7 %psum.38 = f32[16]{0:T(128)S(1)} all-reduce(f32[16]{0:T(128)S(1)} %psum.37), channel_id=1, replica_groups=mesh['dp_0'=4,'dp_1'=4,'expert'=8,'tensor'=2] {'expert'}, use_global_device_ids=true, to_apply=%region_12.13 | all-reduce | flops 16 | bytes 128 | tf_op jit(solution)/shard_map/psum | solution.py:29
  297.9 11.9 %psum.39 = f32[16]{0:T(128)S(1)} all-reduce(f32[16]{0:T(128)S(1)} %psum.38), channel_id=1, replica_groups=mesh['dp_0'=4,'dp_1'=4,'expert'=8,'tensor'=2] {'tensor'}, use_global_device_ids=true, to_apply=%region_13.14 | all-reduce | flops 16 | bytes 128 | tf_op jit(solution)/shard_map/psum | solution.py:29
  309.8 0.0 copy-done.6
  309.8 0.5 convert_divide_fusion
  (5 shorter events, 0.0 us)
Async XLA Ops:
  7.2 2.2 copy-start
  7.2 99.1 %all-gather.2.cloned.1.call-start = ((), (), s32[]{:S(2)}) async-start(), calls=%async_computation.4 | async-start | bytes 8912896 | tf_op jit(solution)/shard_map/all_gather | solution.py:63
  34.4 211.6 %reduce-scatter.2.cloned.1.call-start = ((), (), s32[]{:S(2)}) async-start(), calls=%async_computation.5 | async-start | bytes 17825792 | tf_op jit(solution)/shard_map/reduce_scatter | solution.py:70
  130.3 0.7 copy-start.4
  130.3 1.0 copy-start.2
  130.3 4.1 %copy-start.5 = (s32[64]{0:T(128)S(1)}, s32[64]{0:T(128)}, u32[]{:S(2)}) copy-start(s32[64]{0:T(128)} %param.17) | copy-start | bytes 772
  130.3 4.2 %copy-start.3 = (s32[16,2]{0,1:T(2,128)S(1)}, s32[16,2]{0,1:T(2,128)}, u32[]{:S(2)}) copy-start(s32[16,2]{0,1:T(2,128)} %param.15) | copy-start | bytes 388
  134.5 175.3 %copy-start.6 = (s32[16]{0:T(128)}, s32[16]{0:T(128)S(1)}, u32[]{:S(2)}) copy-start(s32[16]{0:T(128)S(1)} %select_reduce_fusion.1) | copy-start | bytes 196
  246.0 25.5 %copy-start.1 = (bf16[16,2048]{1,0:T(8,128)(2,1)S(1)}, bf16[16,2048]{1,0:T(8,128)(2,1)}, u32[]{:S(2)}) copy-start(bf16[16,2048]{1,0:T(8,128)(2,1)} %param.10) | copy-start | bytes 196612
  253.4 17.9 %all-to-all-start.2 = ((bf16[2,8,4,2048]{3,2,0,1:T(4,128)(2,1)}), bf16[2,8,4,2048]{3,2,0,1:T(4,128)(2,1)S(1)}, u32[]{:S(2)}, u32[]{:S(2)}) async-start(bf16[2,8,4,2048]{3,2,0,1:T(4,128)(2,1)} %copy.61), calls=%async_computation.3 | async-start | bytes 524288 | tf_op jit(solution)/shard_map/all_to_all | solution.py:80
Sparse Core Ops, SparseCore 0:
  34.5 71.6 all-gather.1
  130.5 115.4 reduce-scatter.1
where the time goes:
time: 318 us; the launch traced here: 317 us
  waiting for transfers between devices  194 us (61%)
  blocking collectives  68.7 us (22%)
  matrix products  25.9 us (8%)
  between operations  14.2 us (4%)
  starting transfers between devices  6.86 us (2%)
  local copies, waits for them, and re-layouts  5.59 us (2%)
    reduce_scatter x1, waiting for transfers between devices, per_device(): lax.psum_scatter(jnp.dot(hidden, down_w, preferred_element_type=jnp.float...  111 us
    all_gather x1, waiting for transfers between devices, per_device(): every_row = lax.all_gather(whole, DP, axis=0, tiled=True).reshape(-1, D)  71.8 us
    psum x4, blocking collectives, one_axis_at_a_time(): shard = lax.psum(shard, axis)  37.2 us
    all_to_all x1, blocking collectives, per_device(): lax.all_to_all(outgoing, 'expert', split_axis=1, concat_axis=1, tiled=True)  19.3 us
    dot_general x1, matrix products, per_device(): jnp.dot(hidden, down_w, preferred_element_type=jnp.float32)  16.5 us
    all_to_all x1, waiting for transfers between devices, per_device(): lax.all_to_all(results, 'expert', split_axis=1, concat_axis=1, tiled=True)  10.7 us
    dot_general x1, matrix products, per_device(): gate = jnp.dot(every_row, gate_w, preferred_element_type=jnp.float32)  7.52 us
    all_to_all x1, starting transfers between devices, per_device(): lax.all_to_all(results, 'expert', split_axis=1, concat_axis=1, tiled=True)  6.78 us
  transfers between devices with their start and end apart: 3, of which 3 were waited for; matrix products, arithmetic and copies ran while one was open for 0% of the time, Pallas kernels for 0%

commit v1 on v0

--- a/solution.py
+++ b/solution.py
@@ -60,7 +60,9 @@
     arrived = lax.all_to_all(outgoing, "expert", split_axis=1, concat_axis=1, tiled=True)
     whole = lax.all_gather(arrived, "tensor", axis=3, tiled=True)
     whole = whole.reshape(1, slot_rows, D)
-    every_row = lax.all_gather(whole, DP, axis=0, tiled=True).reshape(-1, D)
+    every_row = jnp.concatenate(
+        lax.all_to_all(jnp.stack([whole] * lax.axis_size(DP)), DP, 0, 0), axis=0
+    ).reshape(-1, D)
     gate_w = w_gate[0]
     up_w = w_up[0]
     down_w = w_down[0]

time: 318 us -> 341 us (1.072)
  blocking collectives: 68.7 us -> 172 us
  waiting for transfers between devices: 194 us -> 115 us
  matrix products: 25.9 us -> 22.3 us
  local copies, waits for them, and re-layouts: 5.59 us -> 9.06 us
    all_to_all x0 -> x1, blocking collectives: none -> 102 us  [per_device(): lax.all_to_all(jnp.stack([whole] * lax.axis_size(DP)), DP, 0, 0)]
    all_gather x1 -> x0, waiting for transfers between devices: 71.8 us -> none  [per_device(): every_row = lax.all_gather(whole, DP, axis=0, tiled=True).reshape(-1, D)]
    reduce_scatter x1, waiting for transfers between devices: 111 us -> 104 us  [per_device(): lax.psum_scatter(jnp.dot(hidden, down_w, preferred_element_type=jnp.float...]
    dot_general x1, matrix products: 7.52 us -> 3.99 us  [per_device(): gate = jnp.dot(every_row, gate_w, preferred_element_type=jnp.float32)]
  transfers between devices with their start and end apart: 3 -> 2, of which waited for: 3 -> 2; matrix products, arithmetic and copies ran while one was open for 0% -> 0% of each run, Pallas kernels for 0% -> 0%
where the time goes in v1:
time: 341 us
  blocking collectives  172 us (50%)
  waiting for transfers between devices  115 us (34%)
  matrix products  22.3 us (7%)
  between operations  14.2 us (4%)
  local copies, waits for them, and re-layouts  9.06 us (3%)
  starting transfers between devices  6.81 us (2%)
    reduce_scatter x1, waiting for transfers between devices, per_device(): lax.psum_scatter(jnp.dot(hidden, down_w, preferred_element_type=jnp.float...  104 us
    all_to_all x1, blocking collectives, per_device(): lax.all_to_all(jnp.stack([whole] * lax.axis_size(DP)), DP, 0, 0)  102 us
    psum x4, blocking collectives, one_axis_at_a_time(): shard = lax.psum(shard, axis)  37.2 us
    all_to_all x1, blocking collectives, per_device(): lax.all_to_all(outgoing, 'expert', split_axis=1, concat_axis=1, tiled=True)  19.3 us
    dot_general x1, matrix products, per_device(): jnp.dot(hidden, down_w, preferred_element_type=jnp.float32)  16.5 us
    all_to_all x1, waiting for transfers between devices, per_device(): lax.all_to_all(results, 'expert', split_axis=1, concat_axis=1, tiled=True)  10.7 us
  transfers between devices with their start and end apart: 2, of which 2 were waited for; matrix products, arithmetic and copies ran while one was open for 0% of the time, Pallas kernels for 0%

profile of v1, /device:TPU:1, one launch (start us, length us, event | category | flops | bytes accessed | tf_op | source)
XLA Modules:
  0.0 340.7 jit_solution(12668287122346641736)
XLA Ops:
  7.2 0.0 copy-start
  7.2 0.0 reduce-scatter.2.cloned.1.call-start
  7.2 0.8 copy.53
  8.0 0.1 eq.64
  8.1 0.1 fusion.13
  8.1 0.1 reduce_window_sum.18
  8.2 0.2 select_reduce_fusion
  8.4 0.1 reduce_sum.48
  8.5 0.1 copy.54
  8.6 0.7 fusion.22
  9.3 0.1 fusion.34
  9.3 0.0 copy-done
  9.4 0.3 convolution_convert_fusion
  9.6 0.1 reshape.106
  9.7 0.1 copy.58
  9.8 19.3 %all_to_all.20 = bf16[2,8,4,2048]{3,2,0,1:T(4,128)(2,1)S(1)} all-to-all(bf16[2,8,4,2048]{3,2,0,1:T(4,128)(2,1)S(1)} %copy.58), channel_id=1, replica_groups=mesh['dp_0'=4,'dp_1'=4,'expert'=8,'tensor'=2] {'expert'}, dimensions={1} | all-to-all | bytes 524288 | tf_op jit(solution)/shard_map/all_to_all | solution.py:60
  29.2 4.1 %all_gather.3 = bf16[2,8,4,4096]{3,2,0,1:T(4,128)(2,1)S(1)} all-gather(bf16[2,8,4,2048]{3,2,0,1:T(4,128)(2,1)S(1)} %all_to_all.20), channel_id=1, replica_groups=mesh['dp_0'=4,'dp_1'=4,'expert'=8,'tensor'=2] {'tensor'}, dimensions={3}, use_global_device_ids=true | all-gather | bytes 786432 | tf_op jit(solution)/shard_map/all_gather | solution.py:61
  33.3 0.2 copy.59
  33.5 0.1 stack_reshape.2
  33.6 1.0 stack.9
  34.7 0.0 copy-start.6
  34.7 101.8 %all_to_all.21 = bf16[16,1,64,4096]{3,2,1,0:T(8,128)(2,1)S(1)} all-to-all(bf16[16,1,64,4096]{3,2,1,0:T(8,128)(2,1)S(1)} %stack.9), channel_id=1, replica_groups=mesh['dp_0'=4,'dp_1'=4,'expert'=8,'tensor'=2] {'dp_0','dp_1'}, dimensions={0} | all-to-all | bytes 16777216 | tf_op jit(solution)/shard_map/all_to_all | solution.py:64
  136.5 0.0 copy-start.1
  136.5 3.2 copy-done.1
  139.7 0.0 copy-done.6
  139.7 4.0 %fusion.4 = f32[1024,448]{0,1:T(8,128)S(1)} fusion(bf16[1024,4096]{1,0:T(8,128)(2,1)S(1)} %bitcast.41, bf16[1,4096,448]{1,2,0:T(8,128)(2,1)S(1)} %copy-done.6), kind=kOutput, calls=%fused_computation.4 | convolution fusion | flops 3758096384 | bytes 13893632 | tf_op jit(solution)/shard_map/dot_general | solution.py:69
  143.7 16.5 %fusion = f32[1024,4096]{1,0:T(8,128)} fusion(bf16[1,448,4096]{2,1,0:T(8,128)(2,1)} %param.14, f32[1024,448]{0,1:T(8,128)S(1)} %fusion.4, bf16[1024,4096]{1,0:T(8,128)(2,1)} %bitcast.42, bf16[1,4096,448]{1,2,0:T(8,128)(2,1)} %param.13), kind=kOutput, calls=%fused_computation | convolution fusion | flops 7518945280 | bytes 34340864 | tf_op jit(solution)/shard_map/dot_general | solution.py:73
  160.2 0.0 copy-start.5
  160.2 0.0 copy-start.4
  160.2 0.0 reduce-scatter.2.cloned.1.call-update
  160.3 0.6 copy-done.5
  160.9 0.1 copy.63
  161.0 0.1 reduce-window.8
  161.1 0.1 reduce
  161.2 0.0 copy-done.3
  161.2 0.1 fusion.35
  161.3 3.9 %psum.35 = f32[16,8]{0,1:T(8,128)S(1)} all-reduce(f32[16,8]{0,1:T(8,128)S(1)} %fusion.35), channel_id=1, replica_groups=mesh['dp_0'=4,'dp_1'=4,'expert'=8,'tensor'=2] {'tensor'}, use_global_device_ids=true, to_apply=%region_2.3 | all-reduce | flops 128 | bytes 1024 | tf_op jit(solution)/shard_map/psum | solution.py:40
  165.2 0.0 copy-done.7
  165.2 0.1 select_reduce_fusion.1
  165.3 0.0 copy-done.4
  165.3 0.0 copy-start.8
  165.4 0.2 compare_reduce_fusion
  165.6 103.9 %reduce-scatter.2.cloned.1.call-done = f32[64,4096]{1,0:T(8,128)} async-done(((f32[1024,4096]{1,0:T(8,128)}), f32[64,4096]{1,0:T(8,128)}) %reduce-scatter.2.cloned.1.call-update) | async-done | bytes 1048592 | tf_op jit(solution)/shard_map/reduce_scatter | solution.py:72
  269.4 1.3 copy.71
  270.8 5.2 %all_to_all.22 = f32[2,64,2048]{2,1,0:T(8,128)S(1)} all-to-all(f32[2,64,2048]{2,1,0:T(8,128)S(1)} %bitcast.43), channel_id=1, replica_groups=mesh['dp_0'=4,'dp_1'=4,'expert'=8,'tensor'=2] {'tensor'}, dimensions={0} | all-to-all | bytes 2097152 | tf_op jit(solution)/shard_map/all_to_all | solution.py:23
  276.0 0.1 reduce_sum.50
  276.1 0.1 convert_element_type.37
  276.2 0.8 copy.61
  277.0 6.8 %all-to-all-start.3 = ((bf16[2,8,4,2048]{3,2,0,1:T(4,128)(2,1)}), bf16[2,8,4,2048]{3,2,0,1:T(4,128)(2,1)S(1)}, u32[]{:S(2)}, u32[]{:S(2)}) async-start(bf16[2,8,4,2048]{3,2,0,1:T(4,128)(2,1)} %copy.61), calls=%async_computation.4 | async-start | bytes 524288 | tf_op jit(solution)/shard_map/all_to_all | solution.py:82
  283.8 0.1 copy.65
  283.9 0.2 fusion.14
  284.1 0.1 fusion.11
  284.2 10.7 %all-to-all-done.3 = bf16[2,8,4,2048]{3,2,0,1:T(4,128)(2,1)S(1)} async-done(((bf16[2,8,4,2048]{3,2,0,1:T(4,128)(2,1)}), bf16[2,8,4,2048]{3,2,0,1:T(4,128)(2,1)S(1)}, u32[]{:S(2)}, u32[]{:S(2)}) %all-to-all-start.3) | async-done | bytes 262176 | tf_op jit(solution)/shard_map/all_to_all | solution.py:82
  294.9 0.1 copy.62
  295.0 0.1 reshape.108
  295.0 0.0 copy-done.2
  295.0 1.0 multiply_reduce_fusion
  296.0 0.1 convolution_bitcast_fusion
  296.1 8.0 %psum.36 = f32[16]{0:T(128)S(1)} all-reduce(f32[16]{0:T(128)S(1)} %convolution_bitcast_fusion), channel_id=1, replica_groups=mesh['dp_0'=4,'dp_1'=4,'expert'=8,'tensor'=2] {'dp_0'}, use_global_device_ids=true, to_apply=%region_10.11 | all-reduce | flops 16 | bytes 128 | tf_op jit(solution)/shard_map/psum | solution.py:29
  304.1 6.6 %psum.37 = f32[16]{0:T(128)S(1)} all-reduce(f32[16]{0:T(128)S(1)} %psum.36), channel_id=1, replica_groups=mesh['dp_0'=4,'dp_1'=4,'expert'=8,'tensor'=2] {'dp_1'}, use_global_device_ids=true, to_apply=%region_11.12 | all-reduce | flops 16 | bytes 128 | tf_op jit(solution)/shard_map/psum | solution.py:29
  310.8 10.7 %psum.38 = f32[16]{0:T(128)S(1)} all-reduce(f32[16]{0:T(128)S(1)} %psum.37), channel_id=1, replica_groups=mesh['dp_0'=4,'dp_1'=4,'expert'=8,'tensor'=2] {'expert'}, use_global_device_ids=true, to_apply=%region_12.13 | all-reduce | flops 16 | bytes 128 | tf_op jit(solution)/shard_map/psum | solution.py:29
  321.4 11.9 %psum.39 = f32[16]{0:T(128)S(1)} all-reduce(f32[16]{0:T(128)S(1)} %psum.38), channel_id=1, replica_groups=mesh['dp_0'=4,'dp_1'=4,'expert'=8,'tensor'=2] {'tensor'}, use_global_device_ids=true, to_apply=%region_13.14 | all-reduce | flops 16 | bytes 128 | tf_op jit(solution)/shard_map/psum | solution.py:29
  333.3 0.0 copy-done.8
  333.3 0.5 convert_divide_fusion
  (8 shorter events, 0.1 us)
Async XLA Ops:
  7.2 2.2 copy-start
  7.2 262.2 %reduce-scatter.2.cloned.1.call-start = ((), (), s32[]{:S(2)}) async-start(), calls=%async_computation.5 | async-start | bytes 17825792 | tf_op jit(solution)/shard_map/reduce_scatter | solution.py:72
  34.7 105.0 %copy-start.6 = (bf16[1,4096,448]{1,2,0:T(8,128)(2,1)S(1)}, bf16[1,4096,448]{1,2,0:T(8,128)(2,1)}, u32[]{:S(2)}) copy-start(bf16[1,4096,448]{1,2,0:T(8,128)(2,1)} %param.12) | copy-start | bytes 11010052
  136.5 3.2 copy-start.1
  160.2 0.7 copy-start.5
  160.2 1.0 copy-start.3
  160.2 5.0 %copy-start.7 = (s32[64]{0:T(128)S(1)}, s32[64]{0:T(128)}, u32[]{:S(2)}) copy-start(s32[64]{0:T(128)} %param.17) | copy-start | bytes 772
  160.2 5.1 %copy-start.4 = (s32[16,2]{0,1:T(2,128)S(1)}, s32[16,2]{0,1:T(2,128)}, u32[]{:S(2)}) copy-start(s32[16,2]{0,1:T(2,128)} %param.15) | copy-start | bytes 388
  165.3 168.0 %copy-start.8 = (s32[16]{0:T(128)}, s32[16]{0:T(128)S(1)}, u32[]{:S(2)}) copy-start(s32[16]{0:T(128)S(1)} %select_reduce_fusion.1) | copy-start | bytes 196
  269.4 25.6 %copy-start.2 = (bf16[16,2048]{1,0:T(8,128)(2,1)S(1)}, bf16[16,2048]{1,0:T(8,128)(2,1)}, u32[]{:S(2)}) copy-start(bf16[16,2048]{1,0:T(8,128)(2,1)} %param.10) | copy-start | bytes 196612
  277.0 17.9 %all-to-all-start.3 = ((bf16[2,8,4,2048]{3,2,0,1:T(4,128)(2,1)}), bf16[2,8,4,2048]{3,2,0,1:T(4,128)(2,1)S(1)}, u32[]{:S(2)}, u32[]{:S(2)}) async-start(bf16[2,8,4,2048]{3,2,0,1:T(4,128)(2,1)} %copy.61), calls=%async_computation.4 | async-start | bytes 524288 | tf_op jit(solution)/shard_map/all_to_all | solution.py:82
Sparse Core Ops, SparseCore 0:
  160.4 109.0 reduce-scatter.1
